TPU v7x, 32 devices: a whole 2x2x4 slice. The times are simulated.
32 devices in a mesh: section: 2 (over y), dp: 4 (over x, core), mp: 4 (over z).
Axes of the slice: x: 2, y: 2, z: 4, core: 2. Of those that a mesh axis runs over, the one named last changes fastest.
Arguments:
- patches: bfloat16 [4096, 1280], P(('section', 'dp')), may hold values from -6 to 6
- patch_counts: int32 [16], P(('section', 'dp')), may hold values from 64 to 256, as said below
- dest_rows: int32 [1024], P(('section', 'dp')), may hold values from 0 to 4095, as said below
- qkv_weight: bfloat16 [1280, 3, 1280], P(None, None, 'mp'), may hold values from -1 to 1
- out_weight: bfloat16 [1280, 1280], P('mp'), may hold values from -0.15625 to 0.15625
- attn_gain: bfloat16 [1280], replicated, may hold values from 0.25 to 1.75
- merge_gain: bfloat16 [1280], replicated, may hold values from 0.25 to 1.75
- fc1_weight: bfloat16 [5120, 5120], P('mp', ('section', 'dp')), may hold values from -0.078125 to 0.078125
- fc1_bias: bfloat16 [5120], P(('section', 'dp')), may hold values from -3 to 3
- fc2_weight: bfloat16 [5120, 8192], P(('section', 'dp'), 'mp'), may hold values from -0.078125 to 0.078125
- fc2_bias: bfloat16 [8192], P('mp'), may hold values from -3 to 3
- text_embeds: bfloat16 [4096, 8192], P(('section', 'dp'), 'mp'), may hold values from -6 to 6
- section_hidden: bfloat16 [4096, 8192], P(('section', 'dp'), 'mp'), may hold values from -80 to 80
- llm_gain: bfloat16 [8192], P('mp'), may hold values from 0.25 to 1.75
Outputs:
- sequence_embeds: bfloat16 [4096, 8192], P(('section', 'dp'), 'mp')
- layer_inputs: bfloat16 [4096, 8192], P(('section', 'dp'), 'mp')
Inputs may be any that keep to these rules, and one draw needn't show every extreme that they name: `patch_counts`: multiples of 4; a tile's patches fill the first slots of its block. `dest_rows`: all rows differ. Each group's merged slots form runs of 16 consecutive slots (aligned); a run goes to one sequence slice (row // 512, numbered in section-major order), different runs of a group to different slices. Rows of slots that are not live are never written.
All inputs are finite; a program needn't handle non-finite values.
Results may differ from a plain program's by a relative error of at most 0.0055.
Values may be sent and summed in bfloat16 or wider, within the bound.
A program may use at most 128 MiB of HBM per device.

v0:
```python
import jax
import jax.numpy as jnp
from jax import lax
from jax.sharding import PartitionSpec as P

HEAD_DIM = 80
HID = 8192
vit_eps = 1e-06
llm_eps = 1e-06


def from_behind(value, axis, steps):
    count = lax.axis_size(axis)
    first, last = (max(0, -steps), min(count, count - steps))
    return lax.ppermute(value, axis, [(source, source + steps) for source in range(first, last)])


def layer_norm(values, gain):
    centred = values.astype(jnp.float32)
    centred = centred - jnp.mean(centred, axis=-1, keepdims=True)
    variance = jnp.mean(centred * centred, axis=-1, keepdims=True)
    return centred * lax.rsqrt(variance + vit_eps) * gain.astype(jnp.float32)


def sum_scatter_mp(blocks):
    return lax.psum_scatter(blocks, "mp", scatter_dimension=0, tiled=False).astype(jnp.float32)


def gather_mp(value):
    return lax.all_gather(value, "mp", axis=0, tiled=True)


def total_mp(value):
    return lax.psum(value, "mp")


def gather_groups(value):
    return lax.all_gather(value, ("section", "dp"), axis=0, tiled=True)


def sum_scatter_groups(value):
    return lax.psum_scatter(value, ("section", "dp"), scatter_dimension=0, tiled=True)


def per_device(
    patches,
    patch_counts,
    dest_rows,
    qkv_weight,
    out_weight,
    attn_gain,
    merge_gain,
    fc1_weight,
    fc1_bias,
    fc2_weight,
    fc2_bias,
    text_embeds,
    section_hidden,
    llm_gain,
):
    width = patches.shape[1]
    tile_total = patch_counts.shape[0]
    block_rows = patches.shape[0] // tile_total
    merged_rows = patches.shape[0] // 4
    local_cols = qkv_weight.shape[2]
    local_heads = local_cols // HEAD_DIM
    feature_cols = text_embeds.shape[1]
    seq_rows = text_embeds.shape[0]
    section_count = lax.axis_size("section")
    group_count = section_count * lax.axis_size("dp")
    run_cap = max(2, merged_rows // group_count)
    run_total = merged_rows // run_cap
    run_target = dest_rows.reshape(run_total, run_cap)[:, 0] // seq_rows
    takes = jnp.arange(group_count, dtype=jnp.int32)[:, None] == run_target[None, :]
    slot_in_tile = jnp.arange(merged_rows, dtype=jnp.int32) % (block_rows // 4)
    tile_counts = jnp.repeat(patch_counts, block_rows // 4, total_repeat_length=merged_rows)
    live = slot_in_tile * 4 < tile_counts
    place = jnp.where(live, dest_rows % seq_rows - seq_rows, 0).reshape(run_total, run_cap)
    send_place = jnp.sum(jnp.where(takes[:, :, None], place[None], 0), axis=1) + seq_rows
    got_place = lax.all_to_all(
        send_place, ("section", "dp"), split_axis=0, concat_axis=0, tiled=True
    )
    incoming = from_behind(section_hidden, "section", 1)
    normed_in = layer_norm(patches, attn_gain).astype(jnp.bfloat16)
    projections = jnp.dot(
        normed_in, qkv_weight.reshape(width, 3 * local_cols), preferred_element_type=jnp.float32
    ).astype(jnp.bfloat16)
    projections = projections.reshape(tile_total, block_rows, 3, local_heads, HEAD_DIM)
    query_part = projections[:, :, 0]
    key_part = projections[:, :, 1]
    value_part = projections[:, :, 2]
    scores = jnp.einsum(
        "tqhd,tkhd->thqk", query_part, key_part, preferred_element_type=jnp.float32
    ) * HEAD_DIM ** (-0.5)
    key_live = (
        jnp.arange(block_rows, dtype=jnp.int32)[None, None, None, :]
        < patch_counts[:, None, None, None]
    )
    scores = jnp.where(key_live, scores, -1e30)
    weights = jax.nn.softmax(scores, axis=-1).astype(jnp.bfloat16)
    attended = jnp.einsum(
        "thqk,tkhd->tqhd", weights, value_part, preferred_element_type=jnp.float32
    ).astype(jnp.bfloat16)
    attended = attended.reshape(patches.shape[0], local_cols)
    partial_proj = jnp.dot(attended, out_weight, preferred_element_type=jnp.float32)
    position = lax.axis_index("mp")
    own_patch = lax.dynamic_slice_in_dim(
        patches.reshape(merged_rows, 4, width), position, 1, 1
    ).reshape(merged_rows, width)
    own_proj = sum_scatter_mp(
        partial_proj.astype(jnp.bfloat16).reshape(merged_rows, 4, width).transpose(1, 0, 2)
    )
    block_out = (own_patch.astype(jnp.float32) + own_proj).astype(jnp.bfloat16)
    merge_part = layer_norm(block_out, merge_gain).astype(jnp.bfloat16)
    lane_same = jnp.arange(run_cap)[:, None] == jnp.arange(run_cap)[None, :]
    order = (takes[:, None, :, None] & lane_same[None, :, None, :]).reshape(
        group_count * run_cap, merged_rows
    )
    merge_part = jnp.dot(
        order.astype(jnp.bfloat16), merge_part, preferred_element_type=jnp.float32
    ).astype(jnp.bfloat16)
    slot_rows = group_count * run_cap
    gathered = gather_groups(merge_part)
    gathered = (
        gathered.reshape(group_count, group_count, run_cap, width)
        .transpose(1, 0, 2, 3)
        .reshape(group_count * slot_rows, width)
    )
    first_partial = jnp.dot(gathered, fc1_weight, preferred_element_type=jnp.float32)
    mp_count = lax.axis_size("mp")
    first_total = sum_scatter_mp(
        first_partial.astype(jnp.bfloat16).reshape(mp_count, -1, fc1_weight.shape[1])
    )
    hidden_part = jax.nn.gelu(first_total + fc1_bias.astype(jnp.float32), approximate=False).astype(
        jnp.bfloat16
    )
    hidden = gather_mp(hidden_part)
    second_partial = jnp.dot(hidden, fc2_weight, preferred_element_type=jnp.float32)
    embed_total = sum_scatter_groups(second_partial.astype(jnp.bfloat16)).astype(jnp.float32)
    image_embeds = (embed_total + fc2_bias.astype(jnp.float32)).astype(jnp.bfloat16)
    hits = got_place.reshape(1, -1) == jnp.arange(seq_rows, dtype=jnp.int32)[:, None]
    placed = jnp.dot(
        hits.astype(jnp.bfloat16), image_embeds, preferred_element_type=jnp.float32
    ).astype(jnp.bfloat16)
    sequence_embeds = jnp.where(jnp.any(hits, axis=1)[:, None], placed, text_embeds)
    entering = jnp.where(lax.axis_index("section") == 0, sequence_embeds, incoming).astype(
        jnp.float32
    )
    row_total = total_mp(jnp.sum(entering * entering, axis=1))
    layer_inputs = (
        entering * lax.rsqrt(row_total / HID + llm_eps)[:, None] * llm_gain.astype(jnp.float32)
    ).astype(jnp.bfloat16)
    return (sequence_embeds, layer_inputs)


def solution(mesh):
    in_specs = (
        P(("section", "dp"), None),
        P(("section", "dp")),
        P(("section", "dp")),
        P(None, None, "mp"),
        P("mp", None),
        P(),
        P(),
        P("mp", ("section", "dp")),
        P(("section", "dp")),
        P(("section", "dp"), "mp"),
        P("mp"),
        P(("section", "dp"), "mp"),
        P(("section", "dp"), "mp"),
        P("mp"),
    )
    out_specs = (P(("section", "dp"), "mp"), P(("section", "dp"), "mp"))
    return jax.shard_map(
        per_device, mesh=mesh, in_specs=in_specs, out_specs=out_specs, check_vma=False
    )
```

profile of v0, /device:TPU:4, one launch (start us, length us, event | category | flops | bytes accessed | tf_op | source)
XLA Modules:
  0.0 269.9 jit_solution(1609884030651612214)
XLA Ops:
  7.2 1.7 convert_reduce_fusion
  9.0 0.1 copy-done.1
  9.1 0.5 fusion.7
  9.6 4.3 %convolution_convert_fusion.5 = bf16[512,960]{0,1:T(8,128)(2,1)} fusion(bf16[1280,960]{0,1:T(8,128)(2,1)} %bitcast.95, bf16[512,1280]{1,0:T(8,128)(2,1)S(1)} %copy-done.1, f32[1280]{0:T(1024)S(1)} %convert_element_type.118, f32[512]{0:T(512)S(1)} %add_rsqrt_fusion.1, f32[512]{0:T(512)S(1)} %broadcast_multiply_fusion), kind=kOutput, calls=%fused_computation.24 | convolution fusion | flops 1262059520 | bytes 4760576 | tf_op jit(solution)/shard_map/dot_general | solution.py:85
  13.9 3.3 %reshape.265 = bf16[2,256,3,4,80]{1,0,4,3,2:T(2,128)(2,1)} reshape(bf16[512,960]{0,1:T(8,128)(2,1)} %convolution_convert_fusion.5) | data formatting | bytes 1966080 | tf_op jit(solution)/shard_map/reshape | solution.py:88
  17.2 2.7 %fusion.71 = (bf16[2,256,1,4,80]{1,0,4,3,2:T(2,128)(2,1)S(1)}, bf16[2,256,1,4,80]{1,0,4,3,2:T(2,128)(2,1)S(1)}, bf16[2,256,1,4,80]{1,0,4,3,2:T(2,128)(2,1)}) fusion(bf16[2,256,3,4,80]{1,0,4,3,2:T(2,128)(2,1)} %reshape.265), kind=kLoop, calls=%fused_computation.118 | loop fusion | bytes 1966080 | tf_op jit(solution)/shard_map/slice | solution.py:91
  19.9 0.1 iota_compare_fusion.4
  19.9 3.2 %fusion.73 = (f32[2,4,256]{2,1,0:T(4,128)S(1)}, f32[2,4,256,256]{2,3,1,0:T(8,128)}) fusion(pred[2,256]{1,0:T(4,128)(4,1)S(1)} %iota_compare_fusion.4, bf16[2,256,1,4,80]{1,0,4,3,2:T(2,128)(2,1)} %get-tuple-element.16, bf16[2,256,1,4,80]{1,0,4,3,2:T(2,128)(2,1)S(1)} %get-tuple-element.15), kind=kOutput, calls=%fused_computation.120 | convolution fusion | flops 85983488 | bytes 2761216 | tf_op jit(solution)/shard_map/sub | solution.py:100
  23.1 2.0 fusion.15
  25.1 0.3 copy.50
  25.5 1.9 convolution_convert_fusion.2
  27.4 3.5 %reshape.267 = bf16[128,4,1280]{2,1,0:T(4,128)(2,1)} reshape(bf16[512,1280]{1,0:T(8,128)(2,1)} %convolution_convert_fusion.2) | data formatting | bytes 2621440 | tf_op jit(solution)/shard_map/reshape | solution.py:111
  30.9 2.5 copy.92
  33.4 0.0 all-gather.3.cloned.1.call-start
  33.5 3.5 %reshape.263 = bf16[128,4,1280]{2,1,0:T(4,128)(2,1)} reshape(bf16[512,1280]{1,0:T(8,128)(2,1)} %param.16) | data formatting | bytes 2621440 | tf_op jit(solution)/shard_map/reshape | solution.py:108
  37.0 0.1 reshape.262
  37.1 0.1 slice_reduce_fusion
  37.2 0.1 broadcast_and_fusion
  37.4 0.2 and.61
  37.6 1.9 dynamic-slice_convert_fusion
  39.5 26.6 %reduce-scatter.4.cloned.1.call-done = bf16[1,128,1280]{2,1,0:T(8,128)(2,1)} async-done(((bf16[4,128,1280]{2,1,0:T(8,128)(2,1)}), bf16[1,128,1280]{2,1,0:T(8,128)(2,1)}) %reduce-scatter.4.cloned.1.call-update) | async-done | bytes 327696 | tf_op jit(solution)/shard_map/reduce_scatter | solution.py:26
  66.2 1.2 convert_reduce_fusion.1
  67.4 1.2 fusion.20
  68.6 1.1 convolution_convert_fusion.3
  69.7 28.7 %all-gather.3.cloned.1.call-done = bf16[1024,1280]{1,0:T(8,128)(2,1)} async-done(((bf16[128,1280]{1,0:T(8,128)(2,1)}), bf16[1024,1280]{1,0:T(8,128)(2,1)}) %all-gather.3.cloned.1.call-update) | async-done | bytes 2621456 | tf_op jit(solution)/shard_map/all_gather | solution.py:38
  98.4 2.1 copy.53
  100.5 0.1 copy-done.11
  100.6 3.3 %convolution_convert_fusion.4 = bf16[1024,640]{1,0:T(8,128)(2,1)} fusion(bf16[1024,1280]{1,0:T(8,128)(2,1)S(1)} %bitcast.91, bf16[1280,640]{1,0:T(8,128)(2,1)S(1)} %copy-done.11), kind=kOutput, calls=%fused_computation.23 | convolution fusion | flops 1678376960 | bytes 5570560 | tf_op jit(solution)/shard_map/dot_general | solution.py:129
  103.9 0.2 all-gather.5.cloned.1.call-start
  104.1 31.3 %reduce-scatter.6.cloned.1.call-done = bf16[1,256,640]{2,1,0:T(8,128)(2,1)} async-done(((bf16[4,256,640]{2,1,0:T(8,128)(2,1)}), bf16[1,256,640]{2,1,0:T(8,128)(2,1)}) %reduce-scatter.6.cloned.1.call-update) | async-done | bytes 327696 | tf_op jit(solution)/shard_map/reduce_scatter | solution.py:26
  135.5 3.2 %fusion.27 = bf16[256,640]{1,0:T(8,128)(2,1)} fusion(bf16[1,256,640]{2,1,0:T(8,128)(2,1)} %reduce-scatter.6.cloned.1.call-done, f32[640]{0:T(1024)S(1)} %convert_element_type.142), kind=kLoop, calls=%fused_computation.48 | loop fusion | flops 10977280 | bytes 657920 | tf_op jit(solution)/shard_map/convert_element_type | solution.py:134
  138.7 31.3 %all-gather.5.cloned.1.call-done = bf16[1024,640]{1,0:T(8,128)(2,1)} async-done(((bf16[256,640]{1,0:T(8,128)(2,1)}), bf16[1024,640]{1,0:T(8,128)(2,1)}) %all-gather.5.cloned.1.call-update) | async-done | bytes 1310736 | tf_op jit(solution)/shard_map/all_gather | solution.py:30
  170.0 6.3 %convolution_convert_fusion = bf16[1024,2048]{1,0:T(8,128)(2,1)} fusion(bf16[1024,640]{1,0:T(8,128)(2,1)} %all-gather.5.cloned.1.call-done, bf16[640,2048]{1,0:T(8,128)(2,1)S(1)} %copy-done), kind=kOutput, calls=%fused_computation.6 | convolution fusion | flops 2686451712 | bytes 8126464 | tf_op jit(solution)/shard_map/dot_general | solution.py:138
  176.3 1.4 collective-permute-start
  177.8 0.6 fusion.72
  178.3 1.3 compare_select_fusion.2
  179.6 0.1 broadcast_in_dim.46
  179.7 0.1 select_reduce_fusion
  179.8 0.6 broadcast_add_fusion
  180.4 7.2 %all-to-all-start = ((s32[8,1,16]{2,1,0:T(1,128)}), s32[8,1,16]{2,1,0:T(1,128)S(1)}, u32[]{:S(2)}, u32[]{:S(2)}) async-start(s32[8,1,16]{2,1,0:T(1,128)} %bitcast.3), calls=%async_computation | async-start | bytes 8192 | tf_op jit(solution)/shard_map/all_to_all | solution.py:80
  187.7 54.5 %all-to-all-done = s32[8,1,16]{2,1,0:T(1,128)S(1)} async-done(((s32[8,1,16]{2,1,0:T(1,128)}), s32[8,1,16]{2,1,0:T(1,128)S(1)}, u32[]{:S(2)}, u32[]{:S(2)}) %all-to-all-start) | async-done | bytes 544 | tf_op jit(solution)/shard_map/all_to_all | solution.py:80
  242.2 0.5 broadcast.236
  242.7 0.7 reduce.7
  243.4 0.1 eq.62
  243.5 0.2 fusion.64
  243.7 4.9 %fusion.1 = (f32[512]{0:T(512)S(1)}, bf16[512,2048]{1,0:T(8,128)(2,1)}) fusion(bf16[512,2048]{1,0:T(8,128)(2,1)} %collective-permute-done, pred[]{:T(512)S(6)} %eq.69, bf16[512,2048]{1,0:T(8,128)(2,1)} %param.27, bf16[128,2048]{1,0:T(8,128)(2,1)} %reduce-scatter.8.cloned.1.call-done, f32[2048]{0:T(1024)S(1)} %convert_element_type.146, s32[128]{0:T(128)S(1)} %eq.62, ...), kind=kOutput, calls=%fused_computation.3 | convolution fusion | flops 275578368 | bytes 6827009 | tf_op jit(solution)/shard_map/dot_general | solution.py:142
  248.6 10.7 %psum.7 = f32[512]{0:T(512)S(1)} all-reduce(f32[512]{0:T(512)S(1)} %get-tuple-element.21), channel_id=1, replica_groups=mesh['section'=2,'dp'=4,'mp'=4] {'mp'}, use_global_device_ids=true, to_apply=%region_12.13 | all-reduce | flops 512 | bytes 4096 | tf_op jit(solution)/shard_map/psum | solution.py:34
  259.2 4.1 %fusion.3 = bf16[512,2048]{1,0:T(8,128)(2,1)} fusion(f32[2048]{0:T(1024)S(1)} %convert_element_type.150, f32[512]{0:T(512)S(1)} %add_rsqrt_fusion, bf16[512,2048]{1,0:T(8,128)(2,1)} %get-tuple-element.22, bf16[512,2048]{1,0:T(8,128)(2,1)} %collective-permute-done, pred[]{:T(512)S(6)} %eq.69), kind=kLoop, calls=%fused_computation.5 | loop fusion | flops 5242880 | bytes 6301697 | tf_op jit(solution)/shard_map/convert_element_type | solution.py:152
  (48 shorter events, 0.4 us)
Async XLA Ops:
  7.2 162.9 %copy-start = (bf16[640,2048]{1,0:T(8,128)(2,1)S(1)}, bf16[640,2048]{1,0:T(8,128)(2,1)}, u32[]{:S(2)}) copy-start(bf16[640,2048]{1,0:T(8,128)(2,1)} %param.25) | copy-start | bytes 7864324
  7.2 2.4 copy-start.3
  7.2 59.0 %reduce-scatter.4.cloned.1.call-start = ((), (), s32[]{:S(2)}) async-start(), calls=%async_computation.4 | async-start | bytes 1638400 | tf_op jit(solution)/shard_map/reduce_scatter | solution.py:26
  7.2 1.9 copy-start.1
  13.9 6.0 %copy-start.9 = (s32[2]{0:T(128)S(1)}, s32[2]{0:T(128)}, u32[]{:S(2)}) copy-start(s32[2]{0:T(128)} %param.17) | copy-start | bytes 28
  23.1 2.4 copy-start.12
  33.4 3.6 %copy-start.8 = (s32[128]{0:T(128)S(1)}, s32[128]{0:T(128)}, u32[]{:S(2)}) copy-start(s32[128]{0:T(128)} %param.18) | copy-start | bytes 1540
  33.4 4.2 %copy-start.4 = (bf16[1280]{0:T(1024)(128)(2,1)S(1)}, bf16[1280]{0:T(1024)(128)(2,1)}, u32[]{:S(2)}) copy-start(bf16[1280]{0:T(1024)(128)(2,1)} %param.22) | copy-start | bytes 7684
  33.4 65.0 %all-gather.3.cloned.1.call-start = ((), (), s32[]{:S(2)}) async-start(), calls=%async_computation.5 | async-start | bytes 2949120 | tf_op jit(solution)/shard_map/all_gather | solution.py:38
  66.2 2.4 copy-start.2
  69.7 65.8 %reduce-scatter.6.cloned.1.call-start = ((), (), s32[]{:S(2)}) async-start(), calls=%async_computation.6 | async-start | bytes 1638400 | tf_op jit(solution)/shard_map/reduce_scatter | solution.py:26
  98.4 2.2 copy-start.11
  100.6 3.5 %copy-start.7 = (bf16[640]{0:T(1024)(128)(2,1)S(1)}, bf16[640]{0:T(1024)(128)(2,1)}, u32[]{:S(2)}) copy-start(bf16[640]{0:T(1024)(128)(2,1)} %param.24) | copy-start | bytes 3844
  103.9 66.1 %all-gather.5.cloned.1.call-start = ((), (), s32[]{:S(2)}) async-start(), calls=%async_computation.7 | async-start | bytes 1638400 | tf_op jit(solution)/shard_map/all_gather | solution.py:30
  138.7 105.0 %reduce-scatter.8.cloned.1.call-start = ((), (), s32[]{:S(2)}) async-start(), calls=%async_computation.8 | async-start | bytes 4718592 | tf_op jit(solution)/shard_map/reduce_scatter | solution.py:42
  176.3 2.0 copy-start.10
  176.3 11.3 %copy-start.5 = (bf16[2048]{0:T(1024)(128)(2,1)S(1)}, bf16[2048]{0:T(1024)(128)(2,1)}, u32[]{:S(2)}) copy-start(bf16[2048]{0:T(1024)(128)(2,1)} %param.26) | copy-start | bytes 12292
  176.3 11.4 %copy-start.6 = (bf16[2048]{0:T(1024)(128)(2,1)S(1)}, bf16[2048]{0:T(1024)(128)(2,1)}, u32[]{:S(2)}) copy-start(bf16[2048]{0:T(1024)(128)(2,1)} %param.29) | copy-start | bytes 12292
  176.3 67.3 %collective-permute-start = (bf16[512,2048]{1,0:T(8,128)(2,1)}, bf16[512,2048]{1,0:T(8,128)(2,1)}, u32[]{:S(2)}, u32[]{:S(2)}) collective-permute-start(bf16[512,2048]{1,0:T(8,128)(2,1)} %param.28), channel_id=1, source_target_pairs={{0,16},{1,17},{2,18},{3,19},{4,20},{5,21},{6,22},{7,23},{8,24},{9,... | collective-permute-start | bytes 6291464 | tf_op jit(solution)/shard_map/ppermute | solution.py:15
  180.4 61.8 %all-to-all-start = ((s32[8,1,16]{2,1,0:T(1,128)}), s32[8,1,16]{2,1,0:T(1,128)S(1)}, u32[]{:S(2)}, u32[]{:S(2)}) async-start(s32[8,1,16]{2,1,0:T(1,128)} %bitcast.3), calls=%async_computation | async-start | bytes 8192 | tf_op jit(solution)/shard_map/all_to_all | solution.py:80
Sparse Core Ops, SparseCore 0:
  33.6 32.5 reduce-scatter.3
  69.8 28.5 all-gather.2
  104.0 31.4 reduce-scatter.5
  138.8 31.1 all-gather.4
  176.4 65.5 reduce-scatter.7
where the time goes:
time: 271 us; the launch traced here: 270 us
  waiting for transfers between devices  173 us (64%)
  matrix products  26.9 us (10%)
  local copies, waits for them, and re-layouts  19.9 us (7%)
  other arithmetic  16.9 us (6%)
  between operations  14 us (5%)
  blocking collectives  10.7 us (4%)
  starting transfers between devices  9.03 us (3%)
    reduce_scatter x2, waiting for transfers between devices, sum_scatter_mp(): lax.psum_scatter(blocks, 'mp', scatter_dimension=0, tiled=False)  58 us
    all_to_all x1, waiting for transfers between devices, per_device(): lax.all_to_all(send_place, ('section', 'dp'), split_axis=0, concat_axis=0...  54.5 us
    all_gather x1, waiting for transfers between devices, gather_mp(): return lax.all_gather(value, 'mp', axis=0, tiled=True)  31.3 us
    all_gather x1, waiting for transfers between devices, gather_groups(): return lax.all_gather(value, ('section', 'dp'), axis=0, tiled=True)  28.7 us
    psum x1, blocking collectives, total_mp(): return lax.psum(value, 'mp')  10.7 us
    all_to_all x1, starting transfers between devices, per_device(): lax.all_to_all(send_place, ('section', 'dp'), split_axis=0, concat_axis=0...  7.22 us
    dot_general x1, matrix products, per_device(): jnp.dot(hidden, fc2_weight, preferred_element_type=jnp.float32)  6.27 us
    reshape x2, local copies, waits for them, and re-layouts, per_device(): partial_proj.astype(jnp.bfloat16).reshape(merged_rows, 4, width)  5.99 us
  transfers between devices with their start and end apart: 7, of which 5 were waited for; matrix products, arithmetic and copies ran while one was open for 4% of the time, Pallas kernels for 0%

commit v1 on v0

--- a/solution.py
+++ b/solution.py
@@ -35,7 +35,21 @@
 
 
 def gather_groups(value):
-    return lax.all_gather(value, ("section", "dp"), axis=0, tiled=True)
+
+    def set_the_patch(field):
+        g_now, t1 = (lax.axis_size(("section", "dp")), lax.axis_index(("section", "dp")))
+        even, part_next = (field, 1)
+        while part_next < g_now:
+            clean = lax.ppermute(
+                even, ("section", "dp"), list(map(lambda d: (d, d ^ part_next), range(g_now)))
+            )
+            aux = jnp.concatenate([even, clean], 0)
+            carry = jnp.concatenate([clean, even], 0)
+            even = jnp.where(t1 & part_next == 0, aux, carry)
+            part_next = 2 * part_next
+        return even
+
+    return set_the_patch(value)
 
 
 def sum_scatter_groups(value):

time: 271 us -> 296 us (1.092)
  waiting for transfers between devices: 173 us -> 190 us
  other arithmetic: 16.9 us -> 23.9 us
    ppermute x0 -> x3, waiting for transfers between devices: none -> 47.1 us  [set_the_patch(): lax.ppermute(even, ('section', 'dp'), list(map(lambda d: (d, d ^ part_nex...]
    all_gather x1 -> x0, waiting for transfers between devices: 28.7 us -> none  [gather_groups(): return lax.all_gather(value, ('section', 'dp'), axis=0, tiled=True)]
    select_n x0 -> x3, other arithmetic: none -> 7.02 us  [set_the_patch(): even = jnp.where(t1 & part_next == 0, aux, carry)]
  transfers between devices with their start and end apart: 7 -> 9, of which waited for: 5 -> 7; matrix products, arithmetic and copies ran while one was open for 4% -> 3% of each run, Pallas kernels for 0% -> 0%
where the time goes in v1:
time: 296 us; the launch traced here: 295 us
  waiting for transfers between devices  190 us (64%)
  matrix products  26.9 us (9%)
  other arithmetic  23.9 us (8%)
  local copies, waits for them, and re-layouts  19.1 us (6%)
  between operations  14 us (5%)
  starting transfers between devices  11.1 us (4%)
  blocking collectives  10.7 us (4%)
    reduce_scatter x2, waiting for transfers between devices, sum_scatter_mp(): lax.psum_scatter(blocks, 'mp', scatter_dimension=0, tiled=False)  56.6 us
    all_to_all x1, waiting for transfers between devices, per_device(): lax.all_to_all(send_place, ('section', 'dp'), split_axis=0, concat_axis=0...  54.5 us
    ppermute x3, waiting for transfers between devices, set_the_patch(): lax.ppermute(even, ('section', 'dp'), list(map(lambda d: (d, d ^ part_nex...  47.1 us
    all_gather x1, waiting for transfers between devices, gather_mp(): return lax.all_gather(value, 'mp', axis=0, tiled=True)  31.3 us
    psum x1, blocking collectives, total_mp(): return lax.psum(value, 'mp')  10.7 us
    all_to_all x1, starting transfers between devices, per_device(): lax.all_to_all(send_place, ('section', 'dp'), split_axis=0, concat_axis=0...  7.22 us
    select_n x3, other arithmetic, set_the_patch(): even = jnp.where(t1 & part_next == 0, aux, carry)  7.02 us
    dot_general x1, matrix products, per_device(): jnp.dot(hidden, fc2_weight, preferred_element_type=jnp.float32)  6.27 us
  transfers between devices with their start and end apart: 9, of which 7 were waited for; matrix products, arithmetic and copies ran while one was open for 3% of the time, Pallas kernels for 0%

profile of v1, /device:TPU:4, one launch (start us, length us, event | category | flops | bytes accessed | tf_op | source)
XLA Modules:
  0.0 295.2 jit_solution(18223835804257184597)
XLA Ops:
  7.2 1.7 convert_reduce_fusion
  9.0 0.1 copy-done.1
  9.1 0.5 fusion.7
  9.6 4.3 %convolution_convert_fusion.5 = bf16[512,960]{0,1:T(8,128)(2,1)} fusion(bf16[1280,960]{0,1:T(8,128)(2,1)} %bitcast.95, bf16[512,1280]{1,0:T(8,128)(2,1)S(1)} %copy-done.1, f32[1280]{0:T(1024)S(1)} %convert_element_type.118, f32[512]{0:T(512)S(1)} %add_rsqrt_fusion.1, f32[512]{0:T(512)S(1)} %broadcast_multiply_fusion), kind=kOutput, calls=%fused_computation.25 | convolution fusion | flops 1262059520 | bytes 4760576 | tf_op jit(solution)/shard_map/dot_general | solution.py:99
  13.9 3.3 %reshape.267 = bf16[2,256,3,4,80]{1,0,4,3,2:T(2,128)(2,1)} reshape(bf16[512,960]{0,1:T(8,128)(2,1)} %convolution_convert_fusion.5) | data formatting | bytes 1966080 | tf_op jit(solution)/shard_map/reshape | solution.py:102
  17.2 2.7 fusion.71
  19.9 3.2 %fusion.73 = (f32[2,4,256]{2,1,0:T(4,128)S(1)}, f32[2,4,256,256]{2,3,1,0:T(8,128)}) fusion(pred[2,256]{1,0:T(4,128)(4,1)S(1)} %iota_compare_fusion.4, bf16[2,256,1,4,80]{1,0,4,3,2:T(2,128)(2,1)} %get-tuple-element.16, bf16[2,256,1,4,80]{1,0,4,3,2:T(2,128)(2,1)S(1)} %get-tuple-element.15), kind=kOutput, calls=%fused_computation.123 | convolution fusion | flops 85983488 | bytes 2761216 | tf_op jit(solution)/shard_map/sub | solution.py:114
  23.1 2.0 fusion.15
  25.1 0.3 copy.50
  25.5 1.9 convolution_convert_fusion.2
  27.4 3.5 %reshape.269 = bf16[128,4,1280]{2,1,0:T(4,128)(2,1)} reshape(bf16[512,1280]{1,0:T(8,128)(2,1)} %convolution_convert_fusion.2) | data formatting | bytes 2621440 | tf_op jit(solution)/shard_map/reshape | solution.py:125
  30.9 2.5 copy.92
  33.4 0.2 reduce-scatter.6.cloned.1.call-start
  33.7 3.5 %reshape.265 = bf16[128,4,1280]{2,1,0:T(4,128)(2,1)} reshape(bf16[512,1280]{1,0:T(8,128)(2,1)} %param.16) | data formatting | bytes 2621440 | tf_op jit(solution)/shard_map/reshape | solution.py:122
  37.4 0.1 broadcast_and_fusion
  37.5 0.2 and.74
  37.8 1.9 dynamic-slice_convert_fusion
  39.7 26.4 %reduce-scatter.4.cloned.1.call-done = bf16[1,128,1280]{2,1,0:T(8,128)(2,1)} async-done(((bf16[4,128,1280]{2,1,0:T(8,128)(2,1)}), bf16[1,128,1280]{2,1,0:T(8,128)(2,1)}) %reduce-scatter.4.cloned.1.call-update) | async-done | bytes 327696 | tf_op jit(solution)/shard_map/reduce_scatter | solution.py:26
  66.2 1.2 convert_reduce_fusion.1
  67.4 1.2 fusion.20
  68.6 1.1 convolution_convert_fusion.3
  69.6 2.0 collective-permute-done
  71.6 1.4 maximum_select_fusion.2
  73.0 1.5 collective-permute-start.1
  74.6 15.4 %collective-permute-done.1 = bf16[256,1280]{1,0:T(8,128)(2,1)} collective-permute-done((bf16[256,1280]{1,0:T(8,128)(2,1)S(1)}, bf16[256,1280]{1,0:T(8,128)(2,1)}, u32[]{:S(2)}, u32[]{:S(2)}) %collective-permute-start.1) | collective-permute-done | bytes 655392 | tf_op jit(solution)/shard_map/ppermute | solution.py:43
  90.0 2.7 maximum_select_fusion.1
  92.7 0.5 collective-permute-start.2
  93.2 29.7 %collective-permute-done.2 = bf16[512,1280]{1,0:T(8,128)(2,1)} collective-permute-done((bf16[512,1280]{1,0:T(8,128)(2,1)}, bf16[512,1280]{1,0:T(8,128)(2,1)}, u32[]{:S(2)}, u32[]{:S(2)}) %collective-permute-start.2) | collective-permute-done | bytes 1310752 | tf_op jit(solution)/shard_map/ppermute | solution.py:43
  122.9 2.9 maximum_select_fusion
  125.9 0.2 copy.53
  126.1 1.2 copy-done.11
  127.3 3.3 %convolution_convert_fusion.4 = bf16[1024,640]{1,0:T(8,128)(2,1)} fusion(bf16[1024,1280]{1,0:T(8,128)(2,1)S(1)} %bitcast.91, bf16[1280,640]{1,0:T(8,128)(2,1)S(1)} %copy-done.11), kind=kOutput, calls=%fused_computation.24 | convolution fusion | flops 1678376960 | bytes 5570560 | tf_op jit(solution)/shard_map/dot_general | solution.py:143
  130.7 30.1 %reduce-scatter.6.cloned.1.call-done = bf16[1,256,640]{2,1,0:T(8,128)(2,1)} async-done(((bf16[4,256,640]{2,1,0:T(8,128)(2,1)}), bf16[1,256,640]{2,1,0:T(8,128)(2,1)}) %reduce-scatter.6.cloned.1.call-update) | async-done | bytes 327696 | tf_op jit(solution)/shard_map/reduce_scatter | solution.py:26
  160.8 3.2 %fusion.27 = bf16[256,640]{1,0:T(8,128)(2,1)} fusion(bf16[1,256,640]{2,1,0:T(8,128)(2,1)} %reduce-scatter.6.cloned.1.call-done, f32[640]{0:T(1024)S(1)} %convert_element_type.142), kind=kLoop, calls=%fused_computation.50 | loop fusion | flops 10977280 | bytes 657920 | tf_op jit(solution)/shard_map/convert_element_type | solution.py:148
  164.0 31.3 %all-gather.2.cloned.1.call-done = bf16[1024,640]{1,0:T(8,128)(2,1)} async-done(((bf16[256,640]{1,0:T(8,128)(2,1)}), bf16[1024,640]{1,0:T(8,128)(2,1)}) %all-gather.2.cloned.1.call-update) | async-done | bytes 1310736 | tf_op jit(solution)/shard_map/all_gather | solution.py:30
  195.3 6.3 %convolution_convert_fusion = bf16[1024,2048]{1,0:T(8,128)(2,1)} fusion(bf16[1024,640]{1,0:T(8,128)(2,1)} %all-gather.2.cloned.1.call-done, bf16[640,2048]{1,0:T(8,128)(2,1)S(1)} %copy-done), kind=kOutput, calls=%fused_computation.6 | convolution fusion | flops 2686451712 | bytes 8126464 | tf_op jit(solution)/shard_map/dot_general | solution.py:152
  201.6 1.4 collective-permute-start.3
  203.0 0.6 fusion.72
  203.6 1.3 compare_select_fusion.2
  205.1 0.6 broadcast_add_fusion
  205.7 7.2 %all-to-all-start = ((s32[8,1,16]{2,1,0:T(1,128)}), s32[8,1,16]{2,1,0:T(1,128)S(1)}, u32[]{:S(2)}, u32[]{:S(2)}) async-start(s32[8,1,16]{2,1,0:T(1,128)} %bitcast.3), calls=%async_computation | async-start | bytes 8192 | tf_op jit(solution)/shard_map/all_to_all | solution.py:94
  213.0 54.5 %all-to-all-done = s32[8,1,16]{2,1,0:T(1,128)S(1)} async-done(((s32[8,1,16]{2,1,0:T(1,128)}), s32[8,1,16]{2,1,0:T(1,128)S(1)}, u32[]{:S(2)}, u32[]{:S(2)}) %all-to-all-start) | async-done | bytes 544 | tf_op jit(solution)/shard_map/all_to_all | solution.py:94
  267.5 0.5 broadcast.239
  268.0 0.7 reduce.7
  268.8 0.2 fusion.64
  269.0 4.9 %fusion.1 = (f32[512]{0:T(512)S(1)}, bf16[512,2048]{1,0:T(8,128)(2,1)}) fusion(bf16[512,2048]{1,0:T(8,128)(2,1)} %collective-permute-done.3, pred[]{:T(512)S(6)} %eq.81, bf16[512,2048]{1,0:T(8,128)(2,1)} %param.27, bf16[128,2048]{1,0:T(8,128)(2,1)} %reduce-scatter.8.cloned.1.call-done, f32[2048]{0:T(1024)S(1)} %convert_element_type.146, s32[128]{0:T(128)S(1)} %eq.71, ...), kind=kOutput, calls=%fused_computation.3 | convolution fusion | flops 275578368 | bytes 6827009 | tf_op jit(solution)/shard_map/dot_general | solution.py:156
  273.9 10.7 %psum.7 = f32[512]{0:T(512)S(1)} all-reduce(f32[512]{0:T(512)S(1)} %get-tuple-element.21), channel_id=1, replica_groups=mesh['section'=2,'dp'=4,'mp'=4] {'mp'}, use_global_device_ids=true, to_apply=%region_12.13 | all-reduce | flops 512 | bytes 4096 | tf_op jit(solution)/shard_map/psum | solution.py:34
  284.5 4.1 %fusion.3 = bf16[512,2048]{1,0:T(8,128)(2,1)} fusion(f32[2048]{0:T(1024)S(1)} %convert_element_type.150, f32[512]{0:T(512)S(1)} %add_rsqrt_fusion, bf16[512,2048]{1,0:T(8,128)(2,1)} %get-tuple-element.22, bf16[512,2048]{1,0:T(8,128)(2,1)} %collective-permute-done.3, pred[]{:T(512)S(6)} %eq.81), kind=kLoop, calls=%fused_computation.5 | loop fusion | flops 5242880 | bytes 6301697 | tf_op jit(solution)/shard_map/convert_element_type | solution.py:166
  (54 shorter events, 0.9 us)
Async XLA Ops:
  7.2 188.2 %copy-start = (bf16[640,2048]{1,0:T(8,128)(2,1)S(1)}, bf16[640,2048]{1,0:T(8,128)(2,1)}, u32[]{:S(2)}) copy-start(bf16[640,2048]{1,0:T(8,128)(2,1)} %param.25) | copy-start | bytes 7864324
  7.2 2.4 copy-start.3
  7.2 59.0 %reduce-scatter.4.cloned.1.call-start = ((), (), s32[]{:S(2)}) async-start(), calls=%async_computation.4 | async-start | bytes 1638400 | tf_op jit(solution)/shard_map/reduce_scatter | solution.py:26
  7.2 1.9 copy-start.1
  13.9 6.0 %copy-start.9 = (s32[2]{0:T(128)S(1)}, s32[2]{0:T(128)}, u32[]{:S(2)}) copy-start(s32[2]{0:T(128)} %param.17) | copy-start | bytes 28
  23.1 2.4 copy-start.12
  33.4 3.8 %copy-start.8 = (s32[128]{0:T(128)S(1)}, s32[128]{0:T(128)}, u32[]{:S(2)}) copy-start(s32[128]{0:T(128)} %param.18) | copy-start | bytes 1540
  33.4 4.4 %copy-start.4 = (bf16[1280]{0:T(1024)(128)(2,1)S(1)}, bf16[1280]{0:T(1024)(128)(2,1)}, u32[]{:S(2)}) copy-start(bf16[1280]{0:T(1024)(128)(2,1)} %param.22) | copy-start | bytes 7684
  33.4 127.3 %reduce-scatter.6.cloned.1.call-start = ((), (), s32[]{:S(2)}) async-start(), calls=%async_computation.5 | async-start | bytes 1638400 | tf_op jit(solution)/shard_map/reduce_scatter | solution.py:26
  66.2 2.4 copy-start.2
  69.6 2.0 collective-permute-start
  73.0 16.9 %collective-permute-start.1 = (bf16[256,1280]{1,0:T(8,128)(2,1)S(1)}, bf16[256,1280]{1,0:T(8,128)(2,1)}, u32[]{:S(2)}, u32[]{:S(2)}) collective-permute-start(bf16[256,1280]{1,0:T(8,128)(2,1)S(1)} %maximum_select_fusion.2), channel_id=1, source_target_pairs={{0,8},{4,12},{8,0},{12,4},{16,24},{20,28},{24,16},{28,20},{1,9},{5... | collective-permute-start | bytes 1966088 | tf_op jit(solution)/shard_map/ppermute | solution.py:43
  92.7 30.3 %collective-permute-start.2 = (bf16[512,1280]{1,0:T(8,128)(2,1)}, bf16[512,1280]{1,0:T(8,128)(2,1)}, u32[]{:S(2)}, u32[]{:S(2)}) collective-permute-start(bf16[512,1280]{1,0:T(8,128)(2,1)} %maximum_select_fusion.1), channel_id=1, source_target_pairs={{0,16},{4,20},{8,24},{12,28},{16,0},{20,4},{24,8},{28,12},{1,17},{... | collective-permute-start | bytes 3932168 | tf_op jit(solution)/shard_map/ppermute | solution.py:43
  125.9 1.4 copy-start.11
  127.3 3.3 %copy-start.7 = (bf16[640]{0:T(1024)(128)(2,1)S(1)}, bf16[640]{0:T(1024)(128)(2,1)}, u32[]{:S(2)}) copy-start(bf16[640]{0:T(1024)(128)(2,1)} %param.24) | copy-start | bytes 3844
  130.6 64.7 %all-gather.2.cloned.1.call-start = ((), (), s32[]{:S(2)}) async-start(), calls=%async_computation.6 | async-start | bytes 1638400 | tf_op jit(solution)/shard_map/all_gather | solution.py:30
  164.0 105.0 %reduce-scatter.8.cloned.1.call-start = ((), (), s32[]{:S(2)}) async-start(), calls=%async_computation.7 | async-start | bytes 4718592 | tf_op jit(solution)/shard_map/reduce_scatter | solution.py:56
  201.6 2.0 copy-start.10
  201.6 11.3 %copy-start.5 = (bf16[2048]{0:T(1024)(128)(2,1)S(1)}, bf16[2048]{0:T(1024)(128)(2,1)}, u32[]{:S(2)}) copy-start(bf16[2048]{0:T(1024)(128)(2,1)} %param.26) | copy-start | bytes 12292
  201.6 11.4 %copy-start.6 = (bf16[2048]{0:T(1024)(128)(2,1)S(1)}, bf16[2048]{0:T(1024)(128)(2,1)}, u32[]{:S(2)}) copy-start(bf16[2048]{0:T(1024)(128)(2,1)} %param.29) | copy-start | bytes 12292
  201.6 67.3 %collective-permute-start.3 = (bf16[512,2048]{1,0:T(8,128)(2,1)}, bf16[512,2048]{1,0:T(8,128)(2,1)}, u32[]{:S(2)}, u32[]{:S(2)}) collective-permute-start(bf16[512,2048]{1,0:T(8,128)(2,1)} %param.28), channel_id=1, source_target_pairs={{0,16},{1,17},{2,18},{3,19},{4,20},{5,21},{6,22},{7,23},{8,24},{9,... | collective-permute-start | bytes 6291464 | tf_op jit(solution)/shard_map/ppermute | solution.py:15
  205.7 61.8 %all-to-all-start = ((s32[8,1,16]{2,1,0:T(1,128)}), s32[8,1,16]{2,1,0:T(1,128)S(1)}, u32[]{:S(2)}, u32[]{:S(2)}) async-start(s32[8,1,16]{2,1,0:T(1,128)} %bitcast.3), calls=%async_computation | async-start | bytes 8192 | tf_op jit(solution)/shard_map/all_to_all | solution.py:94
Sparse Core Ops, SparseCore 0:
  33.6 32.5 reduce-scatter.3
  130.7 30.0 reduce-scatter.5
  164.1 31.1 all-gather.1
  201.7 65.5 reduce-scatter.7
